TPU v7x, 32 devices: a whole 2x2x4 slice. The times are simulated.
32 devices in a mesh: seg: 8 (over z, core), tok: 4 (over y, x).
Axes of the slice: x: 2, y: 2, z: 4, core: 2. Of those that a mesh axis runs over, the one named last changes fastest.
Arguments:
- queries: bfloat16 [2, 8, 2, 5120, 256], P(None, 'seg', None, 'tok'), may hold values from -6 to 6
- key_vectors: bfloat16 [2, 8, 2, 5120, 256], P(None, 'seg', None, 'tok'), may hold values from -6 to 6
- values: bfloat16 [2, 8, 2, 5120, 256], P(None, 'seg', None, 'tok'), may hold values from -6 to 6
- token_rates: float32 [2, 8, 2, 5120], P(None, 'seg', None, 'tok'), may hold values from 0.05 to 3
- fast_weights: float32 [8, 3, 256, 256], P('seg', None, None, 'tok'), may hold values from -0.375 to 0.375
- momenta: float32 [8, 3, 256, 256], P('seg', None, None, 'tok'), may hold values from -3 to 3
- fresh_weights: float32 [3, 256, 256], P(None, None, 'tok'), may hold values from -0.375 to 0.375
- fresh_momenta: float32 [3, 256, 256], P(None, None, 'tok'), may hold values from -3 to 3
Outputs:
- outputs: bfloat16 [2, 8, 2, 5120, 256], P(None, 'seg', None, 'tok')
- final_weights: float32 [8, 3, 256, 256], P('seg', None, None, 'tok')
- final_momenta: float32 [8, 3, 256, 256], P('seg', None, None, 'tok')
All inputs are finite; a program needn't handle non-finite values.
Results may differ from a plain program's by a relative error of at most 0.033.
Values may be sent and summed in bfloat16 or wider, within the bound.
A program may use at most 64 MiB of HBM per device.

v0:
```python
import jax
import jax.numpy as jnp
from jax import lax
from jax.sharding import PartitionSpec as P

momentum_decay = 0.9
learn_rate = 0.05
epsilon = 1e-06


def shifted(array, axis, by):
    length = lax.axis_size(axis)
    pairs = [(i, i + by) for i in range(length) if 0 <= i + by < length]
    return lax.ppermute(array, axis, pairs)


def silu_parts(pre_gate):
    sigmoid_gate = jax.nn.sigmoid(pre_gate)
    return (pre_gate * sigmoid_gate, sigmoid_gate * (1.0 + pre_gate * (1.0 - sigmoid_gate)))


def local_grads(usable_weights, key_rows, value_rows, rate_rows):
    pre_gate = jnp.dot(key_rows, usable_weights[0], preferred_element_type=jnp.float32)
    pre_up = jnp.dot(key_rows, usable_weights[2], preferred_element_type=jnp.float32)
    active, slope_gate = silu_parts(pre_gate)
    hidden = (active * pre_up).astype(jnp.bfloat16)
    scaled = (rate_rows[:, None] * value_rows.astype(jnp.float32)).astype(jnp.bfloat16)
    back_hidden = -lax.dot_general(
        scaled, usable_weights[1], (((1,), (1,)), ((), ())), preferred_element_type=jnp.float32
    )
    back_gate = (back_hidden * pre_up * slope_gate).astype(jnp.bfloat16)
    back_up = (back_hidden * active).astype(jnp.bfloat16)
    contract_rows = (((0,), (0,)), ((), ()))
    grad_gate = lax.dot_general(
        key_rows, back_gate, contract_rows, preferred_element_type=jnp.float32
    )
    grad_down = -lax.dot_general(hidden, scaled, contract_rows, preferred_element_type=jnp.float32)
    grad_up = lax.dot_general(key_rows, back_up, contract_rows, preferred_element_type=jnp.float32)
    return (jnp.stack([grad_gate, grad_down, grad_up]), jnp.sum(rate_rows * rate_rows))


def update(weights, moment, gradients, rate_total):
    moment = momentum_decay * moment + gradients * lax.rsqrt(rate_total)
    stepped = weights - learn_rate * moment
    rescale = jnp.sqrt(
        jnp.sum(weights * weights, axis=1, keepdims=True)
        / (jnp.sum(stepped * stepped, axis=1, keepdims=True) + epsilon)
    )
    return (stepped * rescale, moment)


def apply_fast(usable_weights, query_rows):
    pre_gate = jnp.dot(query_rows, usable_weights[0], preferred_element_type=jnp.float32)
    pre_up = jnp.dot(query_rows, usable_weights[2], preferred_element_type=jnp.float32)
    hidden = (jax.nn.silu(pre_gate) * pre_up).astype(jnp.bfloat16)
    return jnp.dot(hidden, usable_weights[1], preferred_element_type=jnp.float32).astype(
        jnp.bfloat16
    )


def usable(weights):
    rounded = weights.astype(jnp.bfloat16)
    return lax.all_gather(rounded, "tok", axis=2, tiled=True)


def advance(weights, moment, usable_weights, query_rows, key_rows, value_rows, rate_rows):
    gradients, square = local_grads(usable_weights, key_rows, value_rows, rate_rows)
    gradients = lax.psum_scatter(
        gradients.astype(jnp.bfloat16), "tok", scatter_dimension=2, tiled=True
    ).astype(jnp.float32)
    summed = lax.psum(square, "tok")
    weights, moment = update(weights, moment, gradients, summed)
    usable_weights = usable(weights)
    return (weights, moment, usable_weights, apply_fast(usable_weights, query_rows))


def body(
    queries, key_vectors, values, token_rates, fast_weights, momenta, fresh_weights, fresh_momenta
):
    sections = queries.shape[0]
    blocks = queries.shape[2]
    weights, moment, fresh_start, fresh_moment = (
        fast_weights[0],
        momenta[0],
        fresh_weights,
        fresh_momenta,
    )
    is_first = lax.axis_index("seg") == 0
    results = []
    for wave_step in range(sections):
        if wave_step > 0:
            passed = (
                shifted(weights.astype(jnp.bfloat16), "seg", 1).astype(weights.dtype),
                shifted(moment.astype(jnp.bfloat16), "seg", 1).astype(moment.dtype),
            )
            weights = jnp.where(is_first, fresh_start, passed[0])
            moment = jnp.where(is_first, fresh_moment, passed[1])
        usable_weights = usable(weights)
        for block_index in range(blocks):
            weights, moment, usable_weights, result = advance(
                weights,
                moment,
                usable_weights,
                queries[wave_step, 0, block_index],
                key_vectors[wave_step, 0, block_index],
                values[wave_step, 0, block_index],
                token_rates[wave_step, 0, block_index],
            )
            results.append(result)
    row_count = queries.shape[3]
    head_width = queries.shape[4]
    outputs = jnp.stack(results).reshape(sections, blocks, row_count, head_width)[:, None]
    return (outputs, weights[None], moment[None])


def solution(mesh):
    return jax.shard_map(
        body,
        mesh=mesh,
        in_specs=(
            P(None, "seg", None, "tok", None),
            P(None, "seg", None, "tok", None),
            P(None, "seg", None, "tok", None),
            P(None, "seg", None, "tok"),
            P("seg", None, None, "tok"),
            P("seg", None, None, "tok"),
            P(None, None, "tok"),
            P(None, None, "tok"),
        ),
        out_specs=(
            P(None, "seg", None, "tok", None),
            P("seg", None, None, "tok"),
            P("seg", None, None, "tok"),
        ),
        check_vma=False,
    )
```

profile of v0, /device:TPU:0, one launch (start us, length us, event | category | flops | bytes accessed | tf_op | source)
XLA Modules:
  0.0 212.2 jit_solution(14321896189256100010)
XLA Ops:
  7.2 1.1 bitcast_convert_fusion
  8.3 11.0 %all_gather.18 = bf16[3,256,256]{1,2,0:T(8,128)(2,1)S(1)} all-gather(bf16[3,256,64]{1,2,0:T(8,128)(2,1)S(1)} %bitcast_convert_fusion), channel_id=1, replica_groups=mesh['seg'=8,'tok'=4] {'tok'}, dimensions={2}, use_global_device_ids=true | all-gather | bytes 491520 | tf_op jit(solution)/shard_map/all_gather | solution.py:63
  19.3 1.4 fusion.82
  21.6 1.5 convolution_negate_fusion.3
  23.7 1.9 fusion.43
  25.6 0.7 fusion.32
  26.3 0.8 pad_maximum_fusion.1
  27.8 0.7 multiply_reduce_fusion.7
  28.5 9.6 %all-reduce = (f32[]{:T(128)}, f32[]{:T(128)}, f32[]{:T(128)}, f32[]{:T(128)}) all-reduce(f32[]{:T(128)} %get-tuple-element.34, f32[]{:T(128)} %get-tuple-element.33, f32[]{:T(128)} %get-tuple-element.32, f32[]{:T(128)} %get-tuple-element.31), channel_id=1, replica_groups=mesh['seg'=8,'tok'=4] {'tok'}, use_global_device_ids=true, to_apply=%region_2.0 | all-reduce | flops 4 | bytes 32 | tf_op jit(solution)/shard_map/psum | solution.py:71
  38.8 13.5 %reduce-scatter.5.cloned.1.call-done = bf16[3,256,64]{1,2,0:T(8,128)(2,1)} async-done(((bf16[3,256,256]{1,2,0:T(8,128)(2,1)}), bf16[3,256,64]{1,2,0:T(8,128)(2,1)}) %reduce-scatter.5.cloned.1.call-update) | async-done | bytes 98320 | tf_op jit(solution)/shard_map/reduce_scatter | solution.py:68
  52.3 1.0 multiply_reduce_fusion.6
  53.5 9.9 %all_gather.19 = bf16[3,256,256]{1,2,0:T(8,128)(2,1)S(1)} all-gather(bf16[3,256,64]{1,2,0:T(8,128)(2,1)S(1)} %multiply_convert_fusion.27), channel_id=1, replica_groups=mesh['seg'=8,'tok'=4] {'tok'}, dimensions={2}, use_global_device_ids=true | all-gather | bytes 491520 | tf_op jit(solution)/shard_map/all_gather | solution.py:63
  63.4 1.5 convolution_negate_fusion.2
  65.6 0.6 fusion.35
  66.2 1.9 fusion.42
  68.1 0.7 fusion.34
  68.9 0.8 pad_maximum_fusion.2
  70.4 24.1 %reduce-scatter.7.cloned.1.call-done = bf16[3,256,64]{1,2,0:T(8,128)(2,1)} async-done(((bf16[3,256,256]{1,2,0:T(8,128)(2,1)}), bf16[3,256,64]{1,2,0:T(8,128)(2,1)}) %reduce-scatter.7.cloned.1.call-update) | async-done | bytes 98320 | tf_op jit(solution)/shard_map/reduce_scatter | solution.py:68
  94.5 1.7 multiply_reduce_fusion.4
  96.4 1.3 collective-permute-start
  99.1 10.0 %all_gather.21 = bf16[3,256,256]{1,2,0:T(8,128)(2,1)S(1)} all-gather(bf16[3,256,64]{1,2,0:T(8,128)(2,1)S(1)} %fusion.145), channel_id=1, replica_groups=mesh['seg'=8,'tok'=4] {'tok'}, dimensions={2}, use_global_device_ids=true | all-gather | bytes 491520 | tf_op jit(solution)/shard_map/all_gather | solution.py:63
  109.1 1.5 convolution_negate_fusion.1
  111.9 1.9 fusion.41
  113.8 0.7 fusion.36
  114.6 0.8 pad_maximum_fusion.3
  115.5 2.5 %convolution_bitcast_fusion.13 = f32[1280,256]{1,0:T(8,128)} fusion(bf16[2,1,2,1280,256]{4,3,2,1,0:T(8,128)(2,1)} %param.8, bf16[3,256,256]{1,2,0:T(8,128)(2,1)S(1)} %all_gather.19), kind=kOutput, calls=%fused_computation.20 | convolution fusion | flops 167772160 | bytes 2097152 | tf_op jit(solution)/shard_map/dot_general | solution.py:53
  118.0 3.0 %fusion.8 = bf16[1,1280,256]{2,1,0:T(8,128)(2,1)} fusion(f32[1280,256]{1,0:T(8,128)} %convolution_bitcast_fusion.13, bf16[2,1,2,1280,256]{4,3,2,1,0:T(8,128)(2,1)} %param.8, bf16[3,256,256]{1,2,0:T(8,128)(2,1)S(1)} %all_gather.19), kind=kOutput, calls=%fused_computation.31 | convolution fusion | flops 337838080 | bytes 2883584 | tf_op jit(solution)/shard_map/dot_general | solution.py:56
  121.0 2.3 %collective-permute-start.1 = (bf16[3,256,64]{1,2,0:T(8,128)(2,1)}, bf16[3,256,64]{1,2,0:T(8,128)(2,1)S(1)}, u32[]{:S(2)}, u32[]{:S(2)}) collective-permute-start(bf16[3,256,64]{1,2,0:T(8,128)(2,1)} %get-tuple-element.23), channel_id=1, source_target_pairs={{0,4},{4,8},{8,12},{12,16},{16,20},{20,24},{24,28},{1,5},{5,9},{9,... | collective-permute-start | bytes 294920 | tf_op jit(solution)/shard_map/ppermute | solution.py:14
  123.3 10.1 %all_gather.20 = bf16[3,256,256]{1,2,0:T(8,128)(2,1)S(1)} all-gather(bf16[3,256,64]{1,2,0:T(8,128)(2,1)S(1)} %multiply_convert_fusion.24), channel_id=1, replica_groups=mesh['seg'=8,'tok'=4] {'tok'}, dimensions={2}, use_global_device_ids=true | all-gather | bytes 491520 | tf_op jit(solution)/shard_map/all_gather | solution.py:63
  133.3 2.7 %convolution_bitcast_fusion.9 = f32[1280,256]{1,0:T(8,128)} fusion(bf16[2,1,2,1280,256]{4,3,2,1,0:T(8,128)(2,1)} %param.8, bf16[3,256,256]{1,2,0:T(8,128)(2,1)S(1)} %all_gather.20), kind=kOutput, calls=%fused_computation.14 | convolution fusion | flops 167772160 | bytes 2097152 | tf_op jit(solution)/shard_map/dot_general | solution.py:53
  136.0 7.1 %reduce-scatter.9.cloned.1.call-done = bf16[3,256,64]{1,2,0:T(8,128)(2,1)} async-done(((bf16[3,256,256]{1,2,0:T(8,128)(2,1)}), bf16[3,256,64]{1,2,0:T(8,128)(2,1)}) %reduce-scatter.9.cloned.1.call-update) | async-done | bytes 98320 | tf_op jit(solution)/shard_map/reduce_scatter | solution.py:68
  143.1 1.1 multiply_reduce_fusion.2
  144.4 10.2 %all_gather.22 = bf16[3,256,256]{1,2,0:T(8,128)(2,1)S(1)} all-gather(bf16[3,256,64]{1,2,0:T(8,128)(2,1)S(1)} %multiply_convert_fusion.26), channel_id=1, replica_groups=mesh['seg'=8,'tok'=4] {'tok'}, dimensions={2}, use_global_device_ids=true | all-gather | bytes 491520 | tf_op jit(solution)/shard_map/all_gather | solution.py:63
  154.5 1.5 convolution_negate_fusion
  156.7 0.6 fusion.39
  157.4 1.9 fusion.40
  159.3 0.7 fusion.38
  160.0 0.8 pad_maximum_fusion.4
  160.9 3.2 %fusion.9 = bf16[1,1280,256]{2,1,0:T(8,128)(2,1)} fusion(f32[1280,256]{1,0:T(8,128)} %convolution_bitcast_fusion.9, bf16[2,1,2,1280,256]{4,3,2,1,0:T(8,128)(2,1)} %param.8, bf16[3,256,256]{1,2,0:T(8,128)(2,1)} %copy-done.5), kind=kOutput, calls=%fused_computation.32 | convolution fusion | flops 337838080 | bytes 2883584 | tf_op jit(solution)/shard_map/dot_general | solution.py:56
  164.1 1.4 convolution_bitcast_fusion.5
  165.5 2.8 %fusion.10 = bf16[1,1280,256]{2,1,0:T(8,128)(2,1)} fusion(f32[1280,256]{1,0:T(8,128)} %convolution_bitcast_fusion.5, bf16[2,1,2,1280,256]{4,3,2,1,0:T(8,128)(2,1)S(1)} %copy-done.1, bf16[3,256,256]{1,2,0:T(8,128)(2,1)S(1)} %all_gather.22), kind=kOutput, calls=%fused_computation.33 | convolution fusion | flops 337838080 | bytes 2883584 | tf_op jit(solution)/shard_map/dot_general | solution.py:56
  168.3 17.3 %reduce-scatter.11.cloned.1.call-done = bf16[3,256,64]{1,2,0:T(8,128)(2,1)} async-done(((bf16[3,256,256]{1,2,0:T(8,128)(2,1)}), bf16[3,256,64]{1,2,0:T(8,128)(2,1)}) %reduce-scatter.11.cloned.1.call-update) | async-done | bytes 98320 | tf_op jit(solution)/shard_map/reduce_scatter | solution.py:68
  185.6 1.7 multiply_reduce_fusion
  187.3 0.8 multiply_bitcast_fusion
  188.1 9.9 %all_gather.23 = bf16[3,256,256]{1,2,0:T(8,128)(2,1)S(1)} all-gather(bf16[3,256,64]{1,2,0:T(8,128)(2,1)S(1)} %get-tuple-element.29), channel_id=1, replica_groups=mesh['seg'=8,'tok'=4] {'tok'}, dimensions={2}, use_global_device_ids=true | all-gather | bytes 491520 | tf_op jit(solution)/shard_map/all_gather | solution.py:63
  198.0 1.4 convolution_bitcast_fusion.1
  199.4 2.8 %fusion.11 = bf16[1,1280,256]{2,1,0:T(8,128)(2,1)} fusion(f32[1280,256]{1,0:T(8,128)} %convolution_bitcast_fusion.1, bf16[2,1,2,1280,256]{4,3,2,1,0:T(8,128)(2,1)S(1)} %copy-done.1, bf16[3,256,256]{1,2,0:T(8,128)(2,1)S(1)} %all_gather.23), kind=kOutput, calls=%fused_computation.34 | convolution fusion | flops 337838080 | bytes 2883584 | tf_op jit(solution)/shard_map/dot_general | solution.py:56
  202.2 3.5 %pad_maximum_fusion = bf16[4,1280,256]{2,1,0:T(8,128)(2,1)} fusion(bf16[1,1280,256]{2,1,0:T(8,128)(2,1)} %fusion.11, bf16[1,1280,256]{2,1,0:T(8,128)(2,1)} %fusion.10, bf16[1,1280,256]{2,1,0:T(8,128)(2,1)} %fusion.9, bf16[1,1280,256]{2,1,0:T(8,128)(2,1)} %fusion.8), kind=kLoop, calls=%fused_computation.22 | loop fusion | flops 3932160 | bytes 5242880 | tf_op jit(solution)/shard_map/stack | solution.py:112
  (45 shorter events, 5.4 us)
Async XLA Ops:
  7.2 45.1 %reduce-scatter.5.cloned.1.call-start = ((), (), s32[]{:S(2)}) async-start(), calls=%async_computation.4 | async-start | bytes 491520 | tf_op jit(solution)/shard_map/reduce_scatter | solution.py:68
  7.2 13.5 %copy-start = (bf16[2,1,2,1280,256]{4,3,2,1,0:T(8,128)(2,1)S(1)}, bf16[2,1,2,1280,256]{4,3,2,1,0:T(8,128)(2,1)}, u32[]{:S(2)}) copy-start(bf16[2,1,2,1280,256]{4,3,2,1,0:T(8,128)(2,1)} %param.9) | copy-start | bytes 7864324
  20.8 0.7 copy-start.7
  26.3 26.0 %copy-start.3 = (f32[1,3,256,64]{2,3,1,0:T(8,128)S(1)}, f32[1,3,256,64]{2,3,1,0:T(8,128)}, u32[]{:S(2)}) copy-start(f32[1,3,256,64]{2,3,1,0:T(8,128)} %param.12) | copy-start | bytes 589828
  26.3 26.0 %copy-start.4 = (f32[1,3,256,64]{2,3,1,0:T(8,128)S(1)}, f32[1,3,256,64]{2,3,1,0:T(8,128)}, u32[]{:S(2)}) copy-start(f32[1,3,256,64]{2,3,1,0:T(8,128)} %param.13) | copy-start | bytes 589828
  27.1 67.4 %reduce-scatter.7.cloned.1.call-start = ((), (), s32[]{:S(2)}) async-start(), calls=%async_computation.5 | async-start | bytes 491520 | tf_op jit(solution)/shard_map/reduce_scatter | solution.py:68
  68.1 26.4 %copy-start.6 = (bf16[3,256,64]{1,2,0:T(8,128)(2,1)S(1)}, bf16[3,256,64]{1,2,0:T(8,128)(2,1)}, u32[]{:S(2)}) copy-start(bf16[3,256,64]{1,2,0:T(8,128)(2,1)} %reduce-scatter.5.cloned.1.call-done) | copy-start | bytes 294916
  68.9 30.2 %copy-start.2 = (f32[3,256,64]{1,2,0:T(8,128)S(1)}, f32[3,256,64]{1,2,0:T(8,128)}, u32[]{:S(2)}) copy-start(f32[3,256,64]{1,2,0:T(8,128)} %param.14) | copy-start | bytes 589828
  69.7 73.4 %reduce-scatter.9.cloned.1.call-start = ((), (), s32[]{:S(2)}) async-start(), calls=%async_computation.6 | async-start | bytes 491520 | tf_op jit(solution)/shard_map/reduce_scatter | solution.py:68
  96.4 2.6 %collective-permute-start = (bf16[3,256,64]{1,2,0:T(8,128)(2,1)S(1)}, bf16[3,256,64]{1,2,0:T(8,128)(2,1)S(1)}, u32[]{:S(2)}, u32[]{:S(2)}) collective-permute-start(bf16[3,256,64]{1,2,0:T(8,128)(2,1)S(1)} %multiply_convert_fusion.24), channel_id=1, source_target_pairs={{0,4},{4,8},{8,12},{12,16},{16,20},{20,24},{24,28},{1,5},{5,9},{9,... | collective-permute-start | bytes 294920 | tf_op jit(solution)/shard_map/ppermute | solution.py:14
  115.4 70.2 %reduce-scatter.11.cloned.1.call-start = ((), (), s32[]{:S(2)}) async-start(), calls=%async_computation.7 | async-start | bytes 491520 | tf_op jit(solution)/shard_map/reduce_scatter | solution.py:68
  121.0 15.0 %collective-permute-start.1 = (bf16[3,256,64]{1,2,0:T(8,128)(2,1)}, bf16[3,256,64]{1,2,0:T(8,128)(2,1)S(1)}, u32[]{:S(2)}, u32[]{:S(2)}) collective-permute-start(bf16[3,256,64]{1,2,0:T(8,128)(2,1)} %get-tuple-element.23), channel_id=1, source_target_pairs={{0,4},{4,8},{8,12},{12,16},{16,20},{20,24},{24,28},{1,5},{5,9},{9,... | collective-permute-start | bytes 294920 | tf_op jit(solution)/shard_map/ppermute | solution.py:14
  133.3 2.7 %copy-start.5 = (bf16[3,256,256]{1,2,0:T(8,128)(2,1)}, bf16[3,256,256]{1,2,0:T(8,128)(2,1)S(1)}, u32[]{:S(2)}) copy-start(bf16[3,256,256]{1,2,0:T(8,128)(2,1)S(1)} %all_gather.20) | copy-start | bytes 1179652
  160.9 3.2 %copy-start.1 = (bf16[2,1,2,1280,256]{4,3,2,1,0:T(8,128)(2,1)S(1)}, bf16[2,1,2,1280,256]{4,3,2,1,0:T(8,128)(2,1)}, u32[]{:S(2)}) copy-start(bf16[2,1,2,1280,256]{4,3,2,1,0:T(8,128)(2,1)} %param.8) | copy-start | bytes 7864324
Sparse Core Ops, SparseCore 0:
  27.3 24.9 reduce-scatter.4
  69.8 24.6 reduce-scatter.6
  115.5 27.5 reduce-scatter.8
  161.0 24.5 reduce-scatter.10
where the time goes:
time: 213 us; the launch traced here: 212 us
  blocking collectives  70.7 us (33%)
  waiting for transfers between devices  62 us (29%)
  matrix products  42.7 us (20%)
  between operations  16.8 us (8%)
  other arithmetic  15.8 us (7%)
  starting transfers between devices  3.74 us (2%)
    reduce_scatter x4, waiting for transfers between devices, advance(): lax.psum_scatter(gradients.astype(jnp.bfloat16), 'tok', scatter_dimension...  61.9 us
    all_gather x6, blocking collectives, usable(): return lax.all_gather(rounded, 'tok', axis=2, tiled=True)  61.1 us
    dot_general x4, matrix products, apply_fast(): jnp.dot(hidden, usable_weights[1], preferred_element_type=jnp.float32)  11.8 us
    psum x1, blocking collectives, advance(): summed = lax.psum(square, 'tok')  9.65 us
    dot_general x4, matrix products, apply_fast(): jnp.dot(query_rows, usable_weights[0], preferred_element_type=jnp.float32)  8 us
    dot_general x4, matrix products, local_grads(): lax.dot_general(hidden, scaled, contract_rows, preferred_element_type=jnp...  7.57 us
    dot_general x4, matrix products, local_grads(): lax.dot_general(scaled, usable_weights[1], (((1,), (1,)), ((), ())), pref...  5.9 us
    reduce_sum x4, other arithmetic, update(): jnp.sum(stepped * stepped, axis=1, keepdims=True) + epsilon  5.57 us
  transfers between devices with their start and end apart: 6, of which 4 were waited for; matrix products, arithmetic and copies ran while one was open for 8% of the time, Pallas kernels for 0%

commit v1 on v0

v1 whole, which is shorter than its diff:
```python
import functools
import jax
import jax.numpy as jnp
from jax import lax
from jax.experimental import pallas as pl
from jax.experimental.pallas import tpu as pltpu
from jax.sharding import PartitionSpec as P

momentum_decay = 0.9
learn_rate = 0.05
epsilon = 1e-06
LANES = 128
MESH = pl.DeviceIdType.MESH
f32 = jnp.float32
bf16 = jnp.bfloat16


def flip(index, mask):
    out, bit = index, 1
    while bit <= mask:
        if mask & bit:
            out = out + bit * (1 - 2 * lax.rem(index // bit, 2))
        bit *= 2
    return out


def pack(matrix):
    width = matrix.shape[1]
    chunks = LANES // width
    high = matrix.shape[0] // chunks
    return jnp.concatenate([matrix[k * high:(k + 1) * high] for k in range(chunks)], axis=1)


def unpack(piece, width):
    chunks = LANES // width
    return jnp.concatenate([piece[:, k * width:(k + 1) * width] for k in range(chunks)], axis=0)


def sigmoid(x):
    return 0.5 + 0.5 * jnp.tanh(0.5 * x)


def mm(a, b):
    return jnp.dot(a, b, preferred_element_type=f32)


def kernel(
    n, segs, steps, blocks, tile,
    k_hbm, v_hbm, q_hbm, rates, w_in, m_in, fw_in, fm_in,
    out_hbm, w_out, m_out,
    kbuf, vbuf, qbuf, obuf, kt, scaled, scaled_t, hid, bgate, bup, wb, wa,
    wstate, mstate, gsend, grecv, own, ent, msend, mrecv, sq,
    load_sem, store_sem, gs_sem, gr_sem, os_sem, or_sem, es_sem, er_sem, ms_sem, mr_sem,
    qs_sem, qr_sem,
):
    total = steps * blocks
    rows, width_all = kbuf.shape[1], kbuf.shape[2]
    width = width_all // n
    chunks = LANES // width
    high = width_all // chunks
    tiles = rows // tile
    seg = lax.axis_index("seg")
    tok = lax.axis_index("tok")
    first = seg == 0
    last = seg == segs - 1
    peers = [flip(tok, d) for d in range(n)]

    def to_peer(d):
        return {"seg": seg, "tok": peers[d]}

    down = {"seg": lax.rem(seg + 1, segs), "tok": tok}
    up = {"seg": lax.rem(seg + segs - 1, segs), "tok": tok}

    def rcopy(src, dst, send, recv, device):
        return pltpu.make_async_remote_copy(
            src_ref=src, dst_ref=dst, send_sem=send, recv_sem=recv,
            device_id=device, device_id_type=MESH,
        )

    loads = [[
        pltpu.make_async_copy(src.at[b], dst.at[b], load_sem.at[j, b])
        for b in range(total)
    ] for j, (src, dst) in enumerate(((k_hbm, kbuf), (v_hbm, vbuf), (q_hbm, qbuf)))]

    barrier = pltpu.get_barrier_semaphore()
    for d in range(1, n):
        pl.semaphore_signal(barrier, inc=1, device_id=to_peer(d), device_id_type=MESH)

    @pl.when(jnp.logical_not(last))
    def _():
        pl.semaphore_signal(barrier, inc=1, device_id=down, device_id_type=MESH)

    @pl.when(jnp.logical_not(first))
    def _():
        pl.semaphore_signal(barrier, inc=1, device_id=up, device_id_type=MESH)

    for b in range(total):
        loads[0][b].start()
        loads[1][b].start()
    for b in range(total):
        loads[2][b].start()

    for m in range(3):
        wstate[m] = pack(w_in[m])
        mstate[m] = pack(m_in[m])
    ent[0, tok] = wstate[...].astype(bf16)
    all_rates = rates[...]
    sums = jnp.sum(all_rates * all_rates, axis=1, keepdims=True)
    sq[tok] = jnp.broadcast_to(sums, (total, LANES))

    @pl.when(first)
    def _():
        for s in range(1, steps):
            for m in range(3):
                ent[s, tok, m] = pack(fw_in[m]).astype(bf16)

    neighbours = (seg + segs - 1) // segs + (2 * segs - 2 - seg) // segs
    pl.semaphore_wait(barrier, n - 1 + neighbours)

    def ent_copy(s, d, device=None):
        return rcopy(
            ent.at[s, tok], ent.at[s, tok], es_sem.at[s, d], er_sem.at[s, d],
            to_peer(d) if device is None else device,
        )

    def sq_copy(d):
        return rcopy(sq.at[tok], sq.at[tok], qs_sem.at[d], qr_sem.at[d], to_peer(d))

    for d in range(1, n):
        ent_copy(0, d).start()
    for d in range(1, n):
        sq_copy(d).start()

    @pl.when(first)
    def _():
        for s in range(1, steps):
            for d in range(1, n):
                ent_copy(s, d).start()

    def g_copy(b, d):
        return rcopy(
            gsend.at[peers[d]], grecv.at[b, d], gs_sem.at[b, d], gr_sem.at[b, d], to_peer(d)
        )

    def own_copy(b, d):
        return rcopy(
            own.at[b, tok], own.at[b, tok], os_sem.at[b, d], or_sem.at[b, d], to_peer(d)
        )

    def relay_copy(b, s, d):
        return rcopy(
            own.at[b, peers[d]], ent.at[s + 1, peers[d]], es_sem.at[s + 1, d],
            er_sem.at[s + 1, d], down,
        )

    def m_copy(s):
        return rcopy(msend.at[s], mrecv.at[s], ms_sem.at[s], mr_sem.at[s], down)

    def restore(source, slot, target):
        for m in range(3):
            for k in range(chunks):
                target[m, k * high:(k + 1) * high, :] = jnp.concatenate(
                    [
                        source[slot, p, m][:, k * width:(k + 1) * width]
                        for p in range(n)
                    ],
                    axis=1,
                )

    def prepare(b):
        pltpu.make_async_copy(k_hbm.at[b], kbuf.at[b], load_sem.at[0, b]).wait()
        pltpu.make_async_copy(v_hbm.at[b], vbuf.at[b], load_sem.at[1, b]).wait()
        kt[...] = kbuf[b].T
        row = jnp.broadcast_to(rates[pl.ds(b, 1), :], (LANES, rows))
        column = jnp.concatenate([row.T] * (width_all // LANES), axis=1)
        product = (column * vbuf[b].astype(f32)).astype(bf16)
        scaled[...] = product
        scaled_t[...] = product.T

    def gradients(b):
        w1, w2, w3 = wb[0], wb[1], wb[2]

        @pl.loop(0, tiles)
        def _(i):
            at = pl.ds(pl.multiple_of(i * tile, tile), tile)
            keys = kbuf[b, at, :]
            gate = mm(keys, w1)
            up_pre = mm(keys, w3)
            back = lax.dot_general(
                scaled[at, :], w2, (((1,), (1,)), ((), ())), preferred_element_type=f32
            )
            sig = sigmoid(gate)
            act = gate * sig
            slope = sig + act * (1.0 - sig)
            hid[at, :] = (act * up_pre).astype(bf16)
            bgate[at, :] = (back * up_pre * slope).astype(bf16)
            bup[at, :] = (back * act).astype(bf16)

        keys_t = kt[...]
        parts = (
            mm(keys_t, bgate[...]),
            mm(scaled_t[...], hid[...]).T,
            mm(keys_t, bup[...]),
        )
        for m in range(3):
            for p in range(n):
                gsend[p, m] = pack(parts[m][:, p * width:(p + 1) * width]).astype(bf16)

    def column_sum(x):
        t = jnp.broadcast_to(jnp.sum(x * x, axis=0, keepdims=True), (8, LANES))
        shift = width
        while shift < LANES:
            t = t + pltpu.roll(t, shift, 1)
            shift *= 2
        return t[:1]

    def update(b):
        square = sq[0, pl.ds(b, 1), :]
        for p in range(1, n):
            square = square + sq[p, pl.ds(b, 1), :]
        factor = lax.rsqrt(square)
        for m in range(3):
            grad = gsend[tok, m].astype(f32)
            for d in range(1, n):
                grad = grad + grecv[b, d, m].astype(f32)
            moment = momentum_decay * mstate[m] - grad * factor
            weight = wstate[m]
            stepped = weight - learn_rate * moment
            rescale = jnp.sqrt(column_sum(weight) / (column_sum(stepped) + epsilon))
            weight = stepped * rescale
            mstate[m] = moment
            wstate[m] = weight
            own[b, tok, m] = weight.astype(bf16)

    def apply_fast(b):
        pltpu.make_async_copy(q_hbm.at[b], qbuf.at[b], load_sem.at[2, b]).wait()
        restore(own, b, wa)
        w1, w2, w3 = wa[0], wa[1], wa[2]

        @pl.loop(0, tiles)
        def _(i):
            at = pl.ds(pl.multiple_of(i * tile, tile), tile)
            asked = qbuf[b, at, :]
            gate = mm(asked, w1)
            hidden = (gate * sigmoid(gate) * mm(asked, w3)).astype(bf16)
            obuf[b, at, :] = mm(hidden, w2).astype(bf16)

        pltpu.make_async_copy(obuf.at[b], out_hbm.at[b], store_sem.at[b]).start()

    prepare(0)
    for d in range(1, n):
        sq_copy(d).wait_recv()

    @pl.loop(0, total)
    def _(b):
        s = b // blocks
        g = b - s * blocks

        @pl.when(g == 0)
        def _():
            for d in range(1, n):
                ent_copy(s, d).wait_recv()

            @pl.when(jnp.logical_and(s > 0, first))
            def _():
                for m in range(3):
                    wstate[m] = pack(fw_in[m])
                    mstate[m] = pack(fm_in[m])

            @pl.when(jnp.logical_and(s > 0, jnp.logical_not(first)))
            def _():
                relay_copy(b - 1, s - 1, 0).wait_recv()
                m_copy(s - 1).wait_recv()
                wstate[...] = ent[s, tok].astype(f32)
                mstate[...] = mrecv[s - 1].astype(f32)

            restore(ent, s, wb)

        @pl.when(g > 0)
        def _():
            restore(own, b - 1, wb)

        gradients(b)
        for d in range(1, n):
            g_copy(b, d).start()

        @pl.when(g > 0)
        def _():
            apply_fast(b - 1)

        for d in range(1, n):
            g_copy(b, d).wait_recv()
        update(b)
        border = jnp.logical_and(g == blocks - 1, s < steps - 1)
        passing = jnp.logical_and(border, jnp.logical_not(last))

        @pl.when(passing)
        def _():
            relay_copy(b, s, 0).start()

        for d in range(1, n):
            own_copy(b, d).start()

        @pl.when(passing)
        def _():
            msend[s] = mstate[...].astype(bf16)
            m_copy(s).start()

        for d in range(1, n):
            g_copy(b, d).wait_send()

        @pl.when(b < total - 1)
        def _():
            prepare(b + 1)

        for d in range(1, n):
            own_copy(b, d).wait_recv()

            @pl.when(passing)
            def _():
                relay_copy(b, s, d).start()

        @pl.when(g == blocks - 1)
        def _():
            apply_fast(b)

        for d in range(1, n):
            own_copy(b, d).wait_send()

        @pl.when(passing)
        def _():
            for d in range(n):
                relay_copy(b, s, d).wait_send()
            m_copy(s).wait_send()

    for m in range(3):
        w_out[m] = unpack(wstate[m], width)
        m_out[m] = unpack(mstate[m], width)

    for d in range(1, n):
        ent_copy(0, d).wait_send()
        sq_copy(d).wait_send()

    @pl.when(first)
    def _():
        for s in range(1, steps):
            for d in range(1, n):
                ent_copy(s, d).wait_send()

    for b in range(total):
        pltpu.make_async_copy(obuf.at[b], out_hbm.at[b], store_sem.at[b]).wait()


def body(n, segs, queries, keys, values, rates, weights, momenta, fresh_w, fresh_m):
    steps, _, blocks, rows, head = queries.shape
    total = steps * blocks
    width = head // n
    high = 2 * width
    tile = 256 if rows % 256 == 0 else rows
    flat = (total, rows, head)
    piece = (3, high, LANES)
    hbm = pl.BlockSpec(memory_space=pl.ANY)
    vmem = pl.BlockSpec(memory_space=pltpu.VMEM)
    dma = pltpu.SemaphoreType.DMA
    big = (rows, head)
    outs = pl.pallas_call(
        functools.partial(kernel, n, segs, steps, blocks, tile),
        out_shape=(
            jax.ShapeDtypeStruct(flat, bf16),
            jax.ShapeDtypeStruct((3, head, width), f32),
            jax.ShapeDtypeStruct((3, head, width), f32),
        ),
        in_specs=[hbm, hbm, hbm, vmem, vmem, vmem, vmem, vmem],
        out_specs=(hbm, vmem, vmem),
        scratch_shapes=[
            pltpu.VMEM(flat, bf16),
            pltpu.VMEM(flat, bf16),
            pltpu.VMEM(flat, bf16),
            pltpu.VMEM(flat, bf16),
            pltpu.VMEM((head, rows), bf16),
            pltpu.VMEM(big, bf16),
            pltpu.VMEM((head, rows), bf16),
            pltpu.VMEM(big, bf16),
            pltpu.VMEM(big, bf16),
            pltpu.VMEM(big, bf16),
            pltpu.VMEM((3, head, head), bf16),
            pltpu.VMEM((3, head, head), bf16),
            pltpu.VMEM(piece, f32),
            pltpu.VMEM(piece, f32),
            pltpu.VMEM((n,) + piece, bf16),
            pltpu.VMEM((total, n) + piece, bf16),
            pltpu.VMEM((total, n) + piece, bf16),
            pltpu.VMEM((steps, n) + piece, bf16),
            pltpu.VMEM((steps,) + piece, bf16),
            pltpu.VMEM((steps,) + piece, bf16),
            pltpu.VMEM((n, total, LANES), f32),
            dma((3, total)),
            dma((total,)),
            dma((total, n)),
            dma((total, n)),
            dma((total, n)),
            dma((total, n)),
            dma((steps, n)),
            dma((steps, n)),
            dma((steps,)),
            dma((steps,)),
            dma((n,)),
            dma((n,)),
        ],
        compiler_params=pltpu.CompilerParams(
            collective_id=0, has_side_effects=True, vmem_limit_bytes=60 * 1024 * 1024
        ),
    )(
        keys.reshape(flat), values.reshape(flat), queries.reshape(flat),
        rates.reshape(total, rows), weights[0], momenta[0], fresh_w, fresh_m,
    )
    return outs[0].reshape(queries.shape), outs[1][None], outs[2][None]


def solution(mesh):
    n, segs = mesh.shape["tok"], mesh.shape["seg"]
    return jax.shard_map(
        functools.partial(body, n, segs),
        mesh=mesh,
        in_specs=(
            P(None, "seg", None, "tok", None),
            P(None, "seg", None, "tok", None),
            P(None, "seg", None, "tok", None),
            P(None, "seg", None, "tok"),
            P("seg", None, None, "tok"),
            P("seg", None, None, "tok"),
            P(None, None, "tok"),
            P(None, None, "tok"),
        ),
        out_specs=(
            P(None, "seg", None, "tok", None),
            P("seg", None, None, "tok"),
            P("seg", None, None, "tok"),
        ),
        check_vma=False,
    )
```

time: 213 us -> 93.7 us (0.44)
  Pallas kernels: 0 us -> 76.8 us
  blocking collectives: 70.7 us -> 0 us
  waiting for transfers between devices: 62 us -> 0 us
  matrix products: 42.7 us -> 0 us
  between operations: 16.8 us -> 0.64 us
  other arithmetic: 15.8 us -> 0 us
  local copies, waits for them, and re-layouts: 0.45 us -> 15.8 us
  starting transfers between devices: 3.74 us -> 0 us
    pallas_call x0 -> x1, Pallas kernels: none -> 76.8 us  [body(): pl.pallas_call(functools.partial(kernel, n, segs, steps, blocks, tile), o...]
    reduce_scatter x4 -> x0, waiting for transfers between devices: 61.9 us -> none  [advance(): lax.psum_scatter(gradients.astype(jnp.bfloat16), 'tok', scatter_dimension...]
    all_gather x6 -> x0, blocking collectives: 61.1 us -> none  [usable(): return lax.all_gather(rounded, 'tok', axis=2, tiled=True)]
    dot_general x32 -> x0, matrix products: 42.7 us -> none  [the longest x4 11.8 us: apply_fast(): jnp.dot(hidden, usable_weights[1], preferred_element_type=jnp.float32)]
    unnamed x16 -> x7, local copies, waits for them, and re-layouts: 0.39 us -> 14.5 us
    psum x1 -> x0, blocking collectives: 9.65 us -> none  [advance(): summed = lax.psum(square, 'tok')]
    reduce_sum x6 -> x0, other arithmetic: 6.86 us -> none  [the longest x4 5.57 us: update(): jnp.sum(stepped * stepped, axis=1, keepdims=True) + epsilon]
    another operation x5 -> x0, other arithmetic: 6.7 us -> none  [the longest x1 3.5 us: body(): jnp.stack(results).reshape(sections, blocks, row_count, head_width)[:, None]]
  transfers between devices with their start and end apart: 6 -> 0, of which waited for: 4 -> 0; matrix products, arithmetic and copies ran while one was open for 8% -> 0% of each run, Pallas kernels for 0% -> 0%
where the time goes in v1:
time: 93.7 us; the launch traced here: 93.3 us
  Pallas kernels  76.8 us (82%)
  local copies, waits for them, and re-layouts  15.8 us (17%)
    pallas_call x1, Pallas kernels, body(): pl.pallas_call(functools.partial(kernel, n, segs, steps, blocks, tile), o...  76.8 us
    unnamed x7, local copies, waits for them, and re-layouts  14.5 us

profile of v1, /device:TPU:0, one launch (start us, length us, event | category | flops | bytes accessed | tf_op | source)
XLA Modules:
  0.0 93.3 jit_solution(9697066320303454899)
XLA Ops:
  0.6 1.4 %reshape.24.rates = f32[4,1280]{1,0:T(4,128)} reshape(f32[2,1,2,1280]{3,2,1,0:T(2,128)} %param.11) | data formatting | bytes 40960 | tf_op jit(solution)/shard_map/reshape | solution.py:415
  2.0 1.8 %copy.11 = f32[1,3,256,64]{3,2,1,0:T(8,128)} copy(f32[1,3,256,64]{2,3,1,0:T(8,128)} %param.12) | data formatting | bytes 393216 | tf_op args[4]
  3.8 1.8 %copy.12 = f32[1,3,256,64]{3,2,1,0:T(8,128)} copy(f32[1,3,256,64]{2,3,1,0:T(8,128)} %param.13) | data formatting | bytes 393216 | tf_op args[5]
  5.7 1.9 %copy.13.fw_in = f32[3,256,64]{2,1,0:T(8,128)} copy(f32[3,256,64]{1,2,0:T(8,128)} %param.14) | data formatting | bytes 393216 | tf_op args[6]
  7.5 1.9 %copy.14.fm_in = f32[3,256,64]{2,1,0:T(8,128)} copy(f32[3,256,64]{1,2,0:T(8,128)} %param.15) | data formatting | bytes 393216 | tf_op args[7]
  9.4 76.8 %shard_map.103 = (bf16[4,1280,256]{2,1,0:T(8,128)(2,1)}, f32[3,256,64]{2,1,0:T(8,128)}, f32[3,256,64]{2,1,0:T(8,128)}) custom-call(bf16[4,1280,256]{2,1,0:T(8,128)(2,1)} %bitcast.11, bf16[4,1280,256]{2,1,0:T(8,128)(2,1)} %bitcast.12, bf16[4,1280,256]{2,1,0:T(8,128)(2,1)} %bitcast.13, f32[4,1280]{1,0:T(4,128)} %reshape.24.rates, f32[3,256,64]{2,1,0:T(8,128)} %bitcast.14, ...), custom_call_target="tpu_custom_call" | custom-call | tf_op jit(solution)/shard_map/pallas_call | solution.py:366
  86.2 1.8 %copy.16 = f32[1,3,256,64]{2,3,1,0:T(8,128)} copy(f32[1,3,256,64]{3,2,1,0:T(8,128)} %bitcast.17) | data formatting | bytes 393216
  88.1 1.8 %copy.17 = f32[1,3,256,64]{2,3,1,0:T(8,128)} copy(f32[1,3,256,64]{3,2,1,0:T(8,128)} %bitcast.16) | data formatting | bytes 393216
  89.9 3.4 %copy.19 = bf16[2,1,2,1280,256]{4,3,2,1,0:T(8,128)(2,1)} copy(bf16[2,1,2,1280,256]{4,3,2,1,0:T(8,128)(2,1)} %bitcast.10) | data formatting | bytes 5242880

commit v2 on v1

v2 whole, which is shorter than its diff:
```python
import functools
import jax
import jax.numpy as jnp
from jax import lax
from jax.experimental import pallas as pl
from jax.experimental.pallas import tpu as pltpu
from jax.sharding import PartitionSpec as P

momentum_decay = 0.9
learn_rate = 0.05
epsilon = 1e-06
LANES = 128
UNROLL = 5
MESH = pl.DeviceIdType.MESH
f32 = jnp.float32
bf16 = jnp.bfloat16


def flip(index, mask):
    out, bit = index, 1
    while bit <= mask:
        if mask & bit:
            out = out + bit * (1 - 2 * lax.rem(index // bit, 2))
        bit *= 2
    return out


def sigmoid(x):
    return 0.5 + 0.5 * jnp.tanh(0.5 * x)


def mm(a, b):
    return jnp.dot(a, b, preferred_element_type=f32)


def mm_t(a, b):
    return lax.dot_general(a, b, (((1,), (1,)), ((), ())), preferred_element_type=f32)


def kernel(
    n, segs, steps, blocks, tile,
    k_hbm, v_hbm, q_hbm, rates, w_in, m_in, fw_in, fm_in,
    out_hbm, wstate, mstate,
    kbuf, vbuf, qbuf, obuf, kt, scaled, scaled_t, hid, bgate, bup,
    gsend, grecv, bank, msend, mrecv, sq,
    load_sem, store_sem, gs_sem, gr_sem, os_sem, or_sem, es_sem, er_sem, ms_sem, mr_sem,
    qs_sem, qr_sem,
):
    total = steps * blocks
    rows, head = kbuf.shape[1], kbuf.shape[2]
    width = head // n
    tiles = rows // tile
    order = (1, 0, 2)
    around = tuple(range(n - 1, 0, -1))
    seg = lax.axis_index("seg")
    tok = lax.axis_index("tok")
    first = seg == 0
    last = seg == segs - 1
    peers = [flip(tok, d) for d in range(n)]

    def part(p):
        return pl.ds(pl.multiple_of(p * width, width), width)

    mine = part(tok)

    def to_peer(d):
        return {"seg": seg, "tok": peers[d]}

    down = {"seg": lax.rem(seg + 1, segs), "tok": tok}
    up = {"seg": lax.rem(seg + segs - 1, segs), "tok": tok}

    def rcopy(src, dst, send, recv, device):
        return pltpu.make_async_remote_copy(
            src_ref=src, dst_ref=dst, send_sem=send, recv_sem=recv,
            device_id=device, device_id_type=MESH,
        )

    loads = [[
        pltpu.make_async_copy(src.at[b], dst.at[b], load_sem.at[j, b])
        for b in range(total)
    ] for j, (src, dst) in enumerate(((k_hbm, kbuf), (v_hbm, vbuf), (q_hbm, qbuf)))]

    barrier = pltpu.get_barrier_semaphore()
    for d in range(1, n):
        pl.semaphore_signal(barrier, inc=1, device_id=to_peer(d), device_id_type=MESH)

    @pl.when(jnp.logical_not(last))
    def _():
        pl.semaphore_signal(barrier, inc=1, device_id=down, device_id_type=MESH)

    @pl.when(jnp.logical_not(first))
    def _():
        pl.semaphore_signal(barrier, inc=1, device_id=up, device_id_type=MESH)

    for b in range(total):
        loads[0][b].start()
        loads[1][b].start()
    for b in range(total):
        loads[2][b].start()

    wstate[...] = w_in[...]
    mstate[...] = m_in[...]
    for m in range(3):
        bank[total, m, mine, :] = w_in[m].astype(bf16)
    for s in range(steps):
        drawn = rates[s]
        sums = jnp.sum(drawn * drawn, axis=1, keepdims=True)
        sq[tok, s] = jnp.broadcast_to(sums, (blocks, LANES))

    @pl.when(first)
    def _():
        for s in range(1, steps):
            for m in range(3):
                bank[total + s, m, mine, :] = fw_in[m].astype(bf16)

    neighbours = (seg + segs - 1) // segs + (2 * segs - 2 - seg) // segs
    pl.semaphore_wait(barrier, n - 1 + neighbours)

    def ent_copy(s, d, m):
        place = bank.at[total + s, m, mine, :]
        return rcopy(place, place, es_sem.at[s, d, m], er_sem.at[s, d, m], to_peer(d))

    def sq_copy(d):
        return rcopy(sq.at[tok], sq.at[tok], qs_sem.at[d], qr_sem.at[d], to_peer(d))

    for m in order:
        for d in around:
            ent_copy(0, d, m).start()
    for d in around:
        sq_copy(d).start()

    @pl.when(first)
    def _():
        for s in range(1, steps):
            for m in order:
                for d in around:
                    ent_copy(s, d, m).start()

    def g_copy(b, d, m):
        return rcopy(
            gsend.at[m, part(peers[d]), :], grecv.at[b, d, m],
            gs_sem.at[b, d, m], gr_sem.at[b, d, m], to_peer(d),
        )

    def own_copy(b, d, m):
        place = bank.at[b, m, mine, :]
        return rcopy(place, place, os_sem.at[b, d, m], or_sem.at[b, d, m], to_peer(d))

    def relay_copy(b, s, d, m):
        piece = part(peers[d])
        return rcopy(
            bank.at[b, m, piece, :], bank.at[total + s + 1, m, piece, :],
            es_sem.at[s + 1, d, m], er_sem.at[s + 1, d, m], down,
        )

    def m_copy(s):
        return rcopy(msend.at[s], mrecv.at[s], ms_sem.at[s], mr_sem.at[s], down)

    def prepare(b):
        pltpu.make_async_copy(k_hbm.at[b], kbuf.at[b], load_sem.at[0, b]).wait()
        pltpu.make_async_copy(v_hbm.at[b], vbuf.at[b], load_sem.at[1, b]).wait()
        kt[...] = kbuf[b].T
        s = b // blocks
        row = jnp.broadcast_to(rates[s, pl.ds(b - s * blocks, 1), :], (LANES, rows))
        column = jnp.concatenate([row.T] * (head // LANES), axis=1)
        product = (column * vbuf[b].astype(f32)).astype(bf16)
        scaled[...] = product
        scaled_t[...] = product.T

    def gradients(b, slot):
        w1, w2, w3 = bank[slot, 0], bank[slot, 1], bank[slot, 2]

        @pl.loop(0, tiles, unroll=UNROLL)
        def _(i):
            at = pl.ds(pl.multiple_of(i * tile, tile), tile)
            keys = kbuf[b, at, :]
            back = mm(scaled[at, :], w2)
            gate = mm_t(keys, w1)
            up_pre = mm_t(keys, w3)
            sig = sigmoid(gate)
            act = gate * sig
            slope = sig + act * (1.0 - sig)
            hid[at, :] = (act * up_pre).astype(bf16)
            bgate[at, :] = (back * up_pre * slope).astype(bf16)
            bup[at, :] = (back * act).astype(bf16)

        for m in order:
            if m == 1:
                grad = mm(scaled_t[...], hid[...])
            else:
                grad = mm(kt[...], (bgate if m == 0 else bup)[...]).T
            gsend[m] = grad.astype(bf16)
            for d in around:
                g_copy(b, d, m).start()

    def update(b, m, factor):
        grad = gsend[m, mine, :].astype(f32)
        for d in range(1, n):
            grad = grad + grecv[b, d, m].astype(f32)
        moment = momentum_decay * mstate[m] - grad * factor
        weight = wstate[m]
        stepped = weight - learn_rate * moment
        before = jnp.sum(weight * weight, axis=1, keepdims=True)
        after = jnp.sum(stepped * stepped, axis=1, keepdims=True)
        weight = stepped * jnp.sqrt(before / (after + epsilon))
        mstate[m] = moment
        wstate[m] = weight
        bank[b, m, mine, :] = weight.astype(bf16)

    def apply_fast(b):
        pltpu.make_async_copy(q_hbm.at[b], qbuf.at[b], load_sem.at[2, b]).wait()
        w1, w2, w3 = bank[b, 0], bank[b, 1], bank[b, 2]

        @pl.loop(0, tiles, unroll=UNROLL)
        def _(i):
            at = pl.ds(pl.multiple_of(i * tile, tile), tile)
            asked = qbuf[b, at, :]
            gate = mm_t(asked, w1)
            hidden = (gate * sigmoid(gate) * mm_t(asked, w3)).astype(bf16)
            obuf[b, at, :] = mm_t(hidden, w2).astype(bf16)

        pltpu.make_async_copy(obuf.at[b], out_hbm.at[b], store_sem.at[b]).start()

    prepare(0)
    for d in range(1, n):
        sq_copy(d).wait_recv()

    @pl.loop(0, total)
    def _(b):
        s = b // blocks
        g = b - s * blocks
        inner = (g + blocks - 1) // blocks
        entered = jnp.logical_and(jnp.logical_and(g == 0, s > 0), jnp.logical_not(first))

        @pl.when(g == 0)
        def _():
            for m in order:
                for d in around:
                    ent_copy(s, d, m).wait_recv()

        @pl.when(jnp.logical_and(jnp.logical_and(g == 0, s > 0), first))
        def _():
            wstate[...] = fw_in[...]
            mstate[...] = fm_in[...]

        @pl.when(entered)
        def _():
            for m in order:
                relay_copy(b - 1, s - 1, 0, m).wait_recv()
                wstate[m] = bank[total + s, m, mine, :].astype(f32)

        gradients(b, (total + s) * (1 - inner) + (b - 1) * inner)

        @pl.when(g > 0)
        def _():
            apply_fast(b - 1)

        @pl.when(entered)
        def _():
            m_copy(s - 1).wait_recv()
            mstate[...] = mrecv[s - 1].astype(f32)

        border = jnp.logical_and(g == blocks - 1, s < steps - 1)
        passing = jnp.logical_and(border, jnp.logical_not(last))
        square = sq[0, s, pl.ds(g, 1), :]
        for p in range(1, n):
            square = square + sq[p, s, pl.ds(g, 1), :]
        factor = lax.rsqrt(jnp.concatenate([square] * (head // LANES), axis=1))

        for m in order:
            for d in around:
                g_copy(b, d, m).wait_recv()
            update(b, m, factor)

            @pl.when(passing)
            def _():
                relay_copy(b, s, 0, m).start()

            for d in around:
                own_copy(b, d, m).start()

        @pl.when(passing)
        def _():
            msend[s] = mstate[...].astype(bf16)
            m_copy(s).start()

        for m in order:
            for d in around:
                g_copy(b, d, m).wait_send()

        @pl.when(b < total - 1)
        def _():
            prepare(b + 1)

        for m in order:
            for d in range(1, n):
                own_copy(b, d, m).wait_recv()

                @pl.when(passing)
                def _():
                    relay_copy(b, s, d, m).start()

        @pl.when(g == blocks - 1)
        def _():
            apply_fast(b)

        for m in order:
            for d in around:
                own_copy(b, d, m).wait_send()

        @pl.when(passing)
        def _():
            for m in order:
                for d in range(n):
                    relay_copy(b, s, d, m).wait_send()
            m_copy(s).wait_send()

    for d in around:
        sq_copy(d).wait_send()
        for m in order:
            ent_copy(0, d, m).wait_send()

    @pl.when(first)
    def _():
        for s in range(1, steps):
            for m in order:
                for d in around:
                    ent_copy(s, d, m).wait_send()

    for b in range(total):
        pltpu.make_async_copy(obuf.at[b], out_hbm.at[b], store_sem.at[b]).wait()


def body(n, segs, queries, keys, values, rates, weights, momenta, fresh_w, fresh_m):
    steps, _, blocks, rows, head = queries.shape
    total = steps * blocks
    width = head // n
    tile = 256 if rows % 256 == 0 else rows
    flat = (total, rows, head)
    piece = (3, width, head)
    hbm = pl.BlockSpec(memory_space=pl.ANY)
    vmem = pl.BlockSpec(memory_space=pltpu.VMEM)
    dma = pltpu.SemaphoreType.DMA
    big = (rows, head)
    turned = (head, rows)
    outs = pl.pallas_call(
        functools.partial(kernel, n, segs, steps, blocks, tile),
        out_shape=(
            jax.ShapeDtypeStruct(flat, bf16),
            jax.ShapeDtypeStruct(piece, f32),
            jax.ShapeDtypeStruct(piece, f32),
        ),
        in_specs=[hbm, hbm, hbm, vmem, vmem, vmem, vmem, vmem],
        out_specs=(hbm, vmem, vmem),
        scratch_shapes=[pltpu.VMEM(flat, bf16)] * 4
        + [
            pltpu.VMEM(turned, bf16),
            pltpu.VMEM(big, bf16),
            pltpu.VMEM(turned, bf16),
            pltpu.VMEM(big, bf16),
            pltpu.VMEM(big, bf16),
            pltpu.VMEM(big, bf16),
            pltpu.VMEM((3, head, head), bf16),
            pltpu.VMEM((total, n) + piece, bf16),
            pltpu.VMEM((total + steps, 3, head, head), bf16),
            pltpu.VMEM((steps,) + piece, bf16),
            pltpu.VMEM((steps,) + piece, bf16),
            pltpu.VMEM((n, steps, blocks, LANES), f32),
            dma((3, total)),
            dma((total,)),
            dma((total, n, 3)),
            dma((total, n, 3)),
            dma((total, n, 3)),
            dma((total, n, 3)),
            dma((steps, n, 3)),
            dma((steps, n, 3)),
            dma((steps,)),
            dma((steps,)),
            dma((n,)),
            dma((n,)),
        ],
        compiler_params=pltpu.CompilerParams(
            collective_id=0, has_side_effects=True, vmem_limit_bytes=60 * 1024 * 1024
        ),
    )(
        keys.reshape(flat), values.reshape(flat), queries.reshape(flat), rates[:, 0],
        jnp.swapaxes(weights[0], 1, 2), jnp.swapaxes(momenta[0], 1, 2),
        jnp.swapaxes(fresh_w, 1, 2), jnp.swapaxes(fresh_m, 1, 2),
    )
    return (
        outs[0].reshape(queries.shape),
        jnp.swapaxes(outs[1], 1, 2)[None],
        jnp.swapaxes(outs[2], 1, 2)[None],
    )


def solution(mesh):
    n, segs = mesh.shape["tok"], mesh.shape["seg"]
    return jax.shard_map(
        functools.partial(body, n, segs),
        mesh=mesh,
        in_specs=(
            P(None, "seg", None, "tok", None),
            P(None, "seg", None, "tok", None),
            P(None, "seg", None, "tok", None),
            P(None, "seg", None, "tok"),
            P("seg", None, None, "tok"),
            P("seg", None, None, "tok"),
            P(None, None, "tok"),
            P(None, None, "tok"),
        ),
        out_specs=(
            P(None, "seg", None, "tok", None),
            P("seg", None, None, "tok"),
            P("seg", None, None, "tok"),
        ),
        check_vma=False,
    )
```

time: 93.7 us -> 70.1 us (0.75)
  Pallas kernels: 76.8 us -> 64.5 us
  local copies, waits for them, and re-layouts: 15.8 us -> 4.81 us
    pallas_call x1, Pallas kernels: 76.8 us -> 64.5 us  [body(): pl.pallas_call(functools.partial(kernel, n, segs, steps, blocks, tile), o...]
    unnamed x7, local copies, waits for them, and re-layouts: 14.5 us -> 4.81 us
    reshape x1 -> x0, local copies, waits for them, and re-layouts: 1.36 us -> none  [body(): rates.reshape(total, rows)]
where the time goes in v2:
time: 70.1 us; the launch traced here: 69.9 us
  Pallas kernels  64.5 us (92%)
  local copies, waits for them, and re-layouts  4.81 us (7%)
    pallas_call x1, Pallas kernels, body(): pl.pallas_call(functools.partial(kernel, n, segs, steps, blocks, tile), o...  64.5 us
    unnamed x7, local copies, waits for them, and re-layouts  4.81 us

profile of v2, /device:TPU:0, one launch (start us, length us, event | category | flops | bytes accessed | tf_op | source)
XLA Modules:
  0.0 69.9 jit_solution(2208706062078833167)
XLA Ops:
  0.6 64.5 %shard_map.103 = (bf16[4,1280,256]{2,1,0:T(8,128)(2,1)}, f32[3,64,256]{2,1,0:T(8,128)}, f32[3,64,256]{2,1,0:T(8,128)}) custom-call(bf16[4,1280,256]{2,1,0:T(8,128)(2,1)} %bitcast.22, bf16[4,1280,256]{2,1,0:T(8,128)(2,1)} %bitcast.23, bf16[4,1280,256]{2,1,0:T(8,128)(2,1)} %bitcast.24, f32[2,2,1280]{2,1,0:T(2,128)} %bitcast.31, f32[3,64,256]{2,1,0:T(8,128)} %bitcast.27, ...), custom_call_target="tpu_custom_call" | custom-call | tf_op jit(solution)/shard_map/pallas_call | solution.py:346
  65.1 0.0 copy-start.1
  65.1 0.0 copy-start
  65.1 3.4 %copy.15 = bf16[2,1,2,1280,256]{4,3,2,1,0:T(8,128)(2,1)} copy(bf16[2,1,2,1280,256]{4,3,2,1,0:T(8,128)(2,1)} %bitcast.21) | data formatting | bytes 5242880
  68.6 0.0 copy-done.1
  68.6 0.7 copy.16
  69.2 0.0 copy-done
  69.2 0.7 copy.17
Async XLA Ops:
  65.1 3.5 %copy-start.1 = (f32[3,64,256]{2,1,0:T(8,128)S(1)}, f32[3,64,256]{2,1,0:T(8,128)}, u32[]{:S(2)}) copy-start(f32[3,64,256]{2,1,0:T(8,128)} %get-tuple-element.7) | copy-start | bytes 589828
  65.1 4.1 %copy-start = (f32[3,64,256]{2,1,0:T(8,128)S(1)}, f32[3,64,256]{2,1,0:T(8,128)}, u32[]{:S(2)}) copy-start(f32[3,64,256]{2,1,0:T(8,128)} %get-tuple-element.8) | copy-start | bytes 589828
